TPU v7x, 256 devices: a 2x2x32 block of a 4x8x32 slice. The times are simulated.
256 devices in a mesh: group: 4 (over y, x), col: 64 (over z, core).
Axes of the slice: x: 2, y: 2, z: 32, core: 2. Of those that a mesh axis runs over, the one named last changes fastest.
The devices are a block of a 4x8x32 slice.
Arguments:
- homolog_embedding: bfloat16 [384, 256, 256], P('group', 'col'), parts along dimension 0, may hold values from -6 to 6
- left_factor_matrix: bfloat16 [256, 32], replicated, may hold values from -0.375 to 0.375
- right_factor_matrix: bfloat16 [256, 32], replicated, may hold values from -0.375 to 0.375
- decoder: bfloat16 [1024, 128], replicated, may hold values from -2 to 2
- pair_output_bias: float32 [128], replicated, may hold values from -3 to 3
- pair_output_gradient: bfloat16 [1024, 256, 128], P('group', 'col'), parts along dimension 0, may hold values from -16 to 16
Outputs:
- first_operand_gradient: float32 [384, 256, 32], P('group', 'col'), parts along dimension 0
- second_operand_gradient: float32 [384, 256, 32], P('group', 'col'), parts along dimension 0
- alignment_gradient: bfloat16 [384, 256, 256], P('group', 'col'), parts along dimension 0
There are 4 independent parts, one for each index of `group`. A program takes and returns all parts, laid end to end along the dimension named above; an argument that names none is the same for every part. Nothing has to cross between parts.
All inputs are finite; a program needn't handle non-finite values.
Results may differ from a plain program's by a relative error of at most 0.0083.
Values may be sent and summed in bfloat16 or wider, within the bound.
No kernel may reach another device: no remote copies, remote signals or barrier semaphores. Data moves between devices by JAX's collectives and lax.ppermute only.
A program may use at most 64 MiB of HBM per device.

v0:
```python
import jax
import jax.numpy as jnp
from jax import lax
from jax.experimental import pallas as pl
from jax.experimental.pallas import tpu as pltpu
from jax.sharding import Mesh
from jax.sharding import PartitionSpec as P


INTERPRET = False
TOGETHER = 2


def build_weight(mine_ref, mix, weight_ref, first):
    _, width, rows = mine_ref.shape
    channels = mix.shape[1] // width
    for k in range(TOGETHER):
        made = lax.dot_general(
            mine_ref[first + k], mix, (((0,), (0,)), ((), ())),
            preferred_element_type=jnp.float32,
        ).astype(jnp.bfloat16)
        for c in range(width):
            weight_ref[c * rows : (c + 1) * rows, k * channels : (k + 1) * channels] = made[
                :, c * channels : (c + 1) * channels
            ]


def slopes_of(linear, scale, bias, upstream):
    return (
        upstream.astype(jnp.float32) * 2.0 * jnp.maximum(linear * scale + bias, 0.0)
    ).astype(jnp.bfloat16)


def pull_back(flipped_ref, slopes, mix_ref, spread_ref, channels):
    width = mix_ref.shape[0]
    rows = flipped_ref.shape[0] // width
    back = jnp.dot(flipped_ref[...], slopes, preferred_element_type=jnp.float32).astype(
        jnp.bfloat16
    )
    for k in range(TOGETHER):
        for c in range(width):
            spread_ref[k * rows : (k + 1) * rows, c * channels : (c + 1) * channels] = back[
                c * rows : (c + 1) * rows, k * channels : (k + 1) * channels
            ]
    out = lax.dot_general(
        spread_ref[...], mix_ref[...], (((1,), (1,)), ((), ())),
        preferred_element_type=jnp.float32,
    )
    return out * (1.0 / rows)


def ahead_kernel(near_ref, far_low_ref, far_high_ref, mine_left_ref, mine_right_ref, by_left_ref,
                 by_right_ref, bias_ref, up_ref, out_ref, linear_ref, flipped_ref, all_ref,
                 weight_ref, spread_ref):
    residues, _, rows = mine_left_ref.shape
    channels = bias_ref.shape[1]
    near = near_ref.shape[0]
    half = far_low_ref.shape[0]
    scale = 1.0 / rows
    all_ref[0:near] = near_ref[...]
    all_ref[near : near + half] = far_low_ref[...]
    all_ref[near + half :] = far_high_ref[...]
    flipped_ref[...] = all_ref[...].T
    bias = jnp.concatenate([bias_ref[...]] * TOGETHER, axis=1)
    for first in range(0, residues, TOGETHER):
        span = slice(first * channels, (first + TOGETHER) * channels)
        build_weight(mine_right_ref, by_right_ref[...], weight_ref, first)
        linear = jnp.dot(all_ref[...], weight_ref[...], preferred_element_type=jnp.float32)
        slopes = slopes_of(linear, scale, bias, up_ref[:, span])
        out_ref[first * rows : (first + TOGETHER) * rows] = pull_back(
            flipped_ref, slopes, by_right_ref, spread_ref, channels
        )
        build_weight(mine_left_ref, by_left_ref[...], weight_ref, first)
        linear_ref[:, span] = jnp.dot(
            all_ref[...], weight_ref[...], preferred_element_type=jnp.float32
        )


def behind_kernel(linear_ref, flipped_ref, by_left_ref, bias_ref, up_ref, out_ref, spread_ref):
    channels = bias_ref.shape[1]
    rows = flipped_ref.shape[0] // by_left_ref.shape[0]
    residues = linear_ref.shape[1] // channels
    bias = jnp.concatenate([bias_ref[...]] * TOGETHER, axis=1)
    for first in range(0, residues, TOGETHER):
        span = slice(first * channels, (first + TOGETHER) * channels)
        slopes = slopes_of(linear_ref[:, span], 1.0 / rows, bias, up_ref[:, span])
        out_ref[first * rows : (first + TOGETHER) * rows] = pull_back(
            flipped_ref, slopes, by_left_ref, spread_ref, channels
        )


def ahead_call(near, far_low, far_high, mine_left, mine_right, by_left, by_right, bias, up):
    residues, width, rows = mine_left.shape
    channels = bias.shape[1]
    count = up.shape[0]
    return pl.pallas_call(
        ahead_kernel,
        out_shape=(
            jax.ShapeDtypeStruct((residues * rows, width), jnp.float32),
            jax.ShapeDtypeStruct((count, residues * channels), jnp.float32),
            jax.ShapeDtypeStruct((width * rows, count), jnp.bfloat16),
        ),
        scratch_shapes=[
            pltpu.VMEM((count, width * rows), jnp.bfloat16),
            pltpu.VMEM((width * rows, TOGETHER * channels), jnp.bfloat16),
            pltpu.VMEM((TOGETHER * rows, width * channels), jnp.bfloat16),
        ],
        compiler_params=pltpu.CompilerParams(vmem_limit_bytes=32 * 1024 * 1024),
        cost_estimate=pl.CostEstimate(
            flops=6_000_000_000, bytes_accessed=4_000_000, transcendentals=0
        ),
        interpret=INTERPRET,
        name="pair_ahead",
    )(near, far_low, far_high, mine_left, mine_right, by_left, by_right, bias, up)


def behind_call(linear, flipped, by_left, bias, up):
    width = by_left.shape[0]
    rows = flipped.shape[0] // width
    channels = bias.shape[1]
    residues = linear.shape[1] // channels
    return pl.pallas_call(
        behind_kernel,
        out_shape=jax.ShapeDtypeStruct((residues * rows, width), jnp.float32),
        scratch_shapes=[pltpu.VMEM((TOGETHER * rows, width * channels), jnp.bfloat16)],
        compiler_params=pltpu.CompilerParams(vmem_limit_bytes=32 * 1024 * 1024),
        cost_estimate=pl.CostEstimate(
            flops=2_000_000_000, bytes_accessed=4_000_000, transcendentals=0
        ),
        interpret=INTERPRET,
        name="pair_behind",
    )(linear, flipped, by_left, bias, up)


def steps(
    homolog_embedding,
    left_factor_matrix,
    right_factor_matrix,
    decoder,
    pair_output_bias,
    pair_output_gradient,
):
    rows, local, _ = homolog_embedding.shape
    width = left_factor_matrix.shape[1]
    channels = decoder.shape[1]
    high = lax.axis_size("high")
    chips = high * 2
    core = lax.axis_index("core")
    low = lax.axis_index("low")
    z = ("high", "low")
    pair = 2 * local
    swap = [(0, 1), (1, 0)]
    up = [(k, (k + 1) % chips) for k in range(chips)]
    down = [(k, (k - 1) % chips) for k in range(chips)]

    factors = jnp.concatenate([left_factor_matrix, right_factor_matrix], axis=1)
    operands = jnp.einsum(
        "sje,ek->jks", homolog_embedding, factors, preferred_element_type=jnp.float32
    ).astype(jnp.bfloat16)
    sent = jnp.concatenate([operands[:, :width], operands[:, width:]], axis=0)
    near = lax.all_gather(sent.reshape(pair, width * rows), "high", axis=0, tiled=True)
    half = near.shape[0] // 2
    far_low = lax.ppermute(near[:half], z, up)
    far_high = lax.ppermute(near[half:], z, down)
    turned = lax.all_to_all(pair_output_gradient, z, 0, 0, tiled=True)

    def in_order(x):
        x = x.reshape(high, 2, pair, pair * channels)
        x = jnp.where(low == 0, x, x[:, ::-1])
        return x.transpose(1, 0, 2, 3).reshape(chips * pair, pair * channels)

    operands, _ = lax.optimization_barrier((operands, near))
    partner = lax.ppermute(operands, "core", swap)
    mine_right = jnp.concatenate([operands[:, width:], partner[:, width:]], axis=0)
    mine_left = jnp.where(
        core == 0,
        jnp.concatenate([operands[:, :width], partner[:, :width]], axis=0),
        jnp.concatenate([partner[:, :width], operands[:, :width]], axis=0),
    )
    gradient = pair_output_gradient.reshape(chips, 2, local, local, channels)
    theirs = lax.ppermute(jnp.where(core == 0, gradient[:, 1], gradient[:, 0]), "core", swap)
    ours = jnp.where(core == 0, gradient[:, 0], gradient[:, 1])
    by_column = jnp.concatenate(
        [
            ours.reshape(chips, local, local * channels),
            theirs.reshape(chips, local, local * channels),
        ],
        axis=2,
    )
    blank = jnp.zeros_like(by_column)
    by_column = in_order(jnp.concatenate([by_column, blank], axis=1))

    by_left = decoder.reshape(width, width * channels)
    by_right = (
        decoder.reshape(width, width, channels).transpose(1, 0, 2).reshape(width, width * channels)
    )
    bias = pair_output_bias.reshape(1, channels)
    second, linear, flipped = ahead_call(
        near, far_low, far_high, mine_left, mine_right, by_left, by_right, bias, by_column
    )
    second = second.reshape(2, local, rows, width)
    second = second[0] + lax.ppermute(second[1], "core", swap)

    by_row = (
        turned.reshape(chips, pair, local, channels)
        .transpose(0, 2, 1, 3)
        .reshape(chips, local, pair * channels)
    )
    by_row = in_order(jnp.concatenate([blank, by_row], axis=1))
    first = behind_call(linear, flipped, by_left, bias, by_row)
    first = first.reshape(2, local, rows, width)
    first = jnp.where(core == 0, first[0], first[1]) + lax.ppermute(
        jnp.where(core == 0, first[1], first[0]), "core", swap
    )
    first = first.transpose(1, 0, 2)
    second = second.transpose(1, 0, 2)
    alignment = jnp.einsum(
        "sjk,ek->sje",
        jnp.concatenate([first, second], axis=2).astype(jnp.bfloat16),
        factors,
        preferred_element_type=jnp.float32,
    ).astype(jnp.bfloat16)
    return first, second, alignment


def solution(mesh):
    groups = mesh.shape["group"]
    split = Mesh(
        mesh.devices.reshape(groups, mesh.shape["col"] // 4, 2, 2), ("group", "high", "low", "core")
    )
    tall = P("group", ("high", "low", "core"), None)
    return jax.shard_map(
        steps,
        mesh=split,
        in_specs=(tall, P(), P(), P(), P(), tall),
        out_specs=(tall, tall, tall),
        check_vma=False,
    )
```

profile of v0, /device:TPU:38, one launch (start us, length us, event | category | flops | bytes accessed | tf_op | source)
XLA Modules:
  0.0 134.5 jit_solution(7163140011914674016)
XLA Ops:
  0.6 0.0 copy-start
  0.6 0.0 copy-start.4
  0.7 0.9 copy-done
  1.6 0.9 fusion
  2.5 0.1 reshape.66
  2.7 60.9 %all_gather.3.near_ref = bf16[128,3072]{1,0:T(8,128)(2,1)S(1)} all-gather(bf16[8,3072]{1,0:T(8,128)(2,1)S(1)} %reshape.66), channel_id=1, replica_groups=mesh['group'=4,'high'=16,'low'=2,'core'=2] {'high'}, dimensions={0}, use_global_device_ids=true | all-gather | bytes 835584 | tf_op jit(solution)/shard_map/all_gather | solution.py:161
  63.6 0.0 copy-start.5
  63.6 0.0 collective-permute-start.2
  63.6 11.4 %all-to-all-start = ((bf16[256,4,128]{2,1,0:T(4,128)(2,1)}), bf16[256,4,128]{2,1,0:T(4,128)(2,1)}, u32[]{:S(2)}, u32[]{:S(2)}) async-start(bf16[256,4,128]{2,1,0:T(4,128)(2,1)} %param.11), calls=%async_computation | async-start | bytes 524288 | tf_op jit(solution)/shard_map/all_to_all | solution.py:165
  75.1 0.0 copy-done.4
  75.1 0.1 broadcast_select_fusion
  75.2 0.2 collective-permute-start.3
  75.4 0.9 fusion.14
  76.3 1.2 collective-permute-start
  77.5 2.0 %collective-permute-start.1 = (bf16[64,3072]{1,0:T(8,128)(2,1)}, bf16[64,3072]{1,0:T(8,128)(2,1)S(1)}, u32[]{:S(2)}, u32[]{:S(2)}) collective-permute-start(bf16[64,3072]{1,0:T(8,128)(2,1)} %get-tuple-element.21), channel_id=1, source_target_pairs={{0,62},{2,0},{4,2},{6,4},{8,6},{10,8},{12,10},{14,12},{16,14},{18,... | collective-permute-start | bytes 1179656 | tf_op jit(solution)/shard_map/ppermute | solution.py:164
  79.6 0.1 select_n.63
  79.7 0.0 copy-done.5
  79.7 0.1 reshape.67.by_left_ref
  79.8 0.1 copy.17
  79.9 0.1 copy.35
  80.0 0.0 collective-permute-done.2
  80.1 0.0 copy-start.1
  80.1 0.0 collective-permute-done.3
  80.1 0.1 reshape.72
  80.2 0.2 fusion.5
  80.3 0.1 fusion.3
  80.5 28.3 %collective-permute-done.far_low_ref = bf16[64,3072]{1,0:T(8,128)(2,1)S(1)} collective-permute-done((bf16[64,3072]{1,0:T(8,128)(2,1)}, bf16[64,3072]{1,0:T(8,128)(2,1)S(1)}, u32[]{:S(2)}, u32[]{:S(2)}) %collective-permute-start) | collective-permute-done | bytes 393248 | tf_op jit(solution)/shard_map/ppermute | solution.py:163
  108.8 0.0 collective-permute-done.1.far_high_ref
  108.8 0.0 copy-done.1
  108.8 13.8 %pair_ahead.1 = (f32[768,32]{1,0:T(8,128)S(1)}, f32[256,1024]{1,0:T(8,128)S(1)}, bf16[3072,256]{1,0:T(8,128)(2,1)S(1)}) custom-call(bf16[128,3072]{1,0:T(8,128)(2,1)S(1)} %all_gather.3.near_ref, bf16[64,3072]{1,0:T(8,128)(2,1)S(1)} %collective-permute-done.far_low_ref, bf16[64,3072]{1,0:T(8,128)(2,1)S(1)} %collective-permute-done.1.far_high_ref, ...), custom_call_target="tpu_custom_call" | custom-call | flops 6000000000 | bytes 4000000 | tf_op jit(solution)/shard_map/pair_ahead/pallas_call | solution.py:96
  122.6 0.0 copy-start.2
  122.6 1.2 copy-done.2
  123.8 0.1 copy.25
  123.9 0.4 collective-permute-start.5
  124.2 0.1 copy.26
  124.3 0.0 all-to-all-done
  124.3 1.0 copy.36
  125.3 0.1 reshape.76
  125.4 0.0 copy-start.3
  125.4 0.2 concatenate.35
  125.6 0.1 fusion.4
  125.8 1.1 copy-done.3
  126.8 4.3 %pair_behind.1 = f32[768,32]{1,0:T(8,128)S(1)} custom-call(f32[256,1024]{1,0:T(8,128)S(1)} %get-tuple-element.8.linear_ref, bf16[3072,256]{1,0:T(8,128)(2,1)S(1)} %copy-done.3, bf16[32,4096]{1,0:T(8,128)(2,1)S(1)} %reshape.67.by_left_ref, f32[1,128]{1,0:T(1,128)S(1)} %bitcast.58, bf16[256,1024]{1,0:T(8,128)(2,1)S(1)} %bitcast.55), custom_call_target="tpu_custom_call" | custom-call | flops 2000000000 | bytes 4000000 | tf_op jit(solution)/shard_map/pair_behind/pallas_call | solution.py:122
  131.1 0.0 copy-start.6
  131.1 0.0 copy-start.7
  131.2 0.1 copy.23
  131.3 0.6 collective-permute-start.4
  131.9 0.0 collective-permute-done.5
  131.9 0.6 fusion.13
  132.5 0.1 copy.24
  132.6 0.2 collective-permute-done.4
  132.8 0.6 fusion.12
  133.4 0.0 copy-done.6
  133.4 0.0 copy-done.7
  133.4 0.2 convolution_convert_fusion
  133.7 0.8 copy.27
  (10 shorter events, 0.2 us)
Async XLA Ops:
  0.6 0.9 copy-start
  0.6 74.4 %copy-start.4 = (bf16[256,4,128]{2,1,0:T(4,128)(2,1)S(1)}, bf16[256,4,128]{2,1,0:T(4,128)(2,1)}, u32[]{:S(2)}) copy-start(bf16[256,4,128]{2,1,0:T(4,128)(2,1)} %param.11) | copy-start | bytes 786436
  63.6 16.0 %copy-start.5 = (bf16[1024,128]{1,0:T(8,128)(2,1)S(1)}, bf16[1024,128]{1,0:T(8,128)(2,1)}, u32[]{:S(2)}) copy-start(bf16[1024,128]{1,0:T(8,128)(2,1)} %param.9) | copy-start | bytes 786436
  63.6 16.4 %collective-permute-start.2 = (bf16[4,64,96]{2,1,0:T(8,128)(2,1)S(1)}, bf16[4,64,96]{2,1,0:T(8,128)(2,1)S(1)}, u32[]{:S(2)}, u32[]{:S(2)}) collective-permute-start(bf16[4,64,96]{2,1,0:T(8,128)(2,1)S(1)} %fusion), channel_id=1, source_target_pairs={{0,1},{1,0},{2,3},{3,2},{4,5},{5,4},{6,7},{7,6},{8,9},{9,8},{10,11... | collective-permute-start | bytes 147464 | tf_op jit(solution)/shard_map/ppermute | solution.py:173
  63.6 60.7 %all-to-all-start = ((bf16[256,4,128]{2,1,0:T(4,128)(2,1)}), bf16[256,4,128]{2,1,0:T(4,128)(2,1)}, u32[]{:S(2)}, u32[]{:S(2)}) async-start(bf16[256,4,128]{2,1,0:T(4,128)(2,1)} %param.11), calls=%async_computation | async-start | bytes 524288 | tf_op jit(solution)/shard_map/all_to_all | solution.py:165
  75.2 4.9 %collective-permute-start.3 = (bf16[32,4,4,128]{3,2,1,0:T(4,128)(2,1)S(1)}, bf16[32,4,4,128]{3,2,1,0:T(4,128)(2,1)S(1)}, u32[]{:S(2)}, u32[]{:S(2)}) collective-permute-start(bf16[32,4,4,128]{3,2,1,0:T(4,128)(2,1)S(1)} %get-tuple-element.28), channel_id=1, source_target_pairs={{0,1},{1,0},{2,3},{3,2},{4,5},{5,4},{6,7},{7,6},{8,9},{9,8},{10,11... | collective-permute-start | bytes 393224 | tf_op jit(solution)/shard_map/ppermute | solution.py:181
  76.3 32.4 %collective-permute-start = (bf16[64,3072]{1,0:T(8,128)(2,1)}, bf16[64,3072]{1,0:T(8,128)(2,1)S(1)}, u32[]{:S(2)}, u32[]{:S(2)}) collective-permute-start(bf16[64,3072]{1,0:T(8,128)(2,1)} %get-tuple-element.22), channel_id=1, source_target_pairs={{0,2},{2,4},{4,6},{6,8},{8,10},{10,12},{12,14},{14,16},{16,18},{18... | collective-permute-start | bytes 1179656 | tf_op jit(solution)/shard_map/ppermute | solution.py:163
  77.5 31.2 %collective-permute-start.1 = (bf16[64,3072]{1,0:T(8,128)(2,1)}, bf16[64,3072]{1,0:T(8,128)(2,1)S(1)}, u32[]{:S(2)}, u32[]{:S(2)}) collective-permute-start(bf16[64,3072]{1,0:T(8,128)(2,1)} %get-tuple-element.21), channel_id=1, source_target_pairs={{0,62},{2,0},{4,2},{6,4},{8,6},{10,8},{12,10},{14,12},{16,14},{18,... | collective-permute-start | bytes 1179656 | tf_op jit(solution)/shard_map/ppermute | solution.py:164
  80.1 28.7 %copy-start.1 = (f32[128]{0:T(128)S(1)}, f32[128]{0:T(128)}, u32[]{:S(2)}) copy-start(f32[128]{0:T(128)} %param.10) | copy-start | bytes 1540
  122.6 1.2 copy-start.2
  123.9 8.0 %collective-permute-start.5 = (f32[4,96,32]{1,2,0:T(8,128)S(1)}, f32[4,96,32]{1,2,0:T(8,128)S(1)}, u32[]{:S(2)}, u32[]{:S(2)}) collective-permute-start(f32[4,96,32]{1,2,0:T(8,128)S(1)} %copy.25), channel_id=1, source_target_pairs={{0,1},{1,0},{2,3},{3,2},{4,5},{5,4},{6,7},{7,6},{8,9},{9,8},{10,11... | collective-permute-start | bytes 147464 | tf_op jit(solution)/shard_map/ppermute | solution.py:202
  125.4 1.4 %copy-start.3 = (bf16[3072,256]{1,0:T(8,128)(2,1)S(1)}, bf16[3072,256]{1,0:T(8,128)(2,1)}, u32[]{:S(2)}) copy-start(bf16[3072,256]{1,0:T(8,128)(2,1)} %copy-done.2) | copy-start | bytes 4718596
  131.1 2.3 %copy-start.6 = (bf16[256,32]{0,1:T(8,128)(2,1)S(1)}, bf16[256,32]{0,1:T(8,128)(2,1)}, u32[]{:S(2)}) copy-start(bf16[256,32]{0,1:T(8,128)(2,1)} %param.8) | copy-start | bytes 49156
  131.1 2.3 %copy-start.7 = (bf16[256,32]{0,1:T(8,128)(2,1)S(1)}, bf16[256,32]{0,1:T(8,128)(2,1)}, u32[]{:S(2)}) copy-start(bf16[256,32]{0,1:T(8,128)(2,1)} %param.7) | copy-start | bytes 49156
  131.3 1.5 %collective-permute-start.4 = (f32[4,96,32]{1,2,0:T(8,128)S(1)}, f32[4,96,32]{1,2,0:T(8,128)S(1)}, u32[]{:S(2)}, u32[]{:S(2)}) collective-permute-start(f32[4,96,32]{1,2,0:T(8,128)S(1)} %copy.23), channel_id=1, source_target_pairs={{0,1},{1,0},{2,3},{3,2},{4,5},{5,4},{6,7},{7,6},{8,9},{9,8},{10,11... | collective-permute-start | bytes 147464 | tf_op jit(solution)/shard_map/ppermute | solution.py:212
where the time goes:
time: 136 us; the launch traced here: 135 us
  blocking collectives  60.9 us (45%)
  waiting for transfers between devices  28.5 us (21%)
  Pallas kernels  18.1 us (13%)
  starting transfers between devices  15.9 us (12%)
  local copies, waits for them, and re-layouts  7.18 us (5%)
  other arithmetic  1.89 us (1%)
    all_gather x1, blocking collectives, steps(): lax.all_gather(sent.reshape(pair, width * rows), 'high', axis=0, tiled=True)  60.9 us
    ppermute x1, waiting for transfers between devices, steps(): far_low = lax.ppermute(near[:half], z, up)  28.3 us
    pallas_call x1, Pallas kernels, ahead_call(): pl.pallas_call(ahead_kernel, out_shape=(jax.ShapeDtypeStruct((residues *...  13.8 us
    all_to_all x1, starting transfers between devices, steps(): turned = lax.all_to_all(pair_output_gradient, z, 0, 0, tiled=True)  11.4 us
    pallas_call x1, Pallas kernels, behind_call(): pl.pallas_call(behind_kernel, out_shape=jax.ShapeDtypeStruct((residues *...  4.31 us
    unnamed x18, local copies, waits for them, and re-layouts  4.1 us
  transfers between devices with their start and end apart: 7, of which 2 were waited for; matrix products, arithmetic and copies ran while one was open for 3% of the time, Pallas kernels for 13%

commit v1 on v0

v1 whole, which is shorter than its diff:
```python
import jax
import jax.numpy as jnp
from jax import lax
from jax.experimental import pallas as pl
from jax.experimental.pallas import tpu as pltpu
from jax.sharding import Mesh
from jax.sharding import PartitionSpec as P


INTERPRET = False
TOGETHER = 2


def build_weight(mine_ref, mix, weight_ref, first):
    _, width, rows = mine_ref.shape
    channels = mix.shape[1] // width
    for k in range(TOGETHER):
        made = lax.dot_general(
            mine_ref[first + k], mix, (((0,), (0,)), ((), ())),
            preferred_element_type=jnp.float32,
        ).astype(jnp.bfloat16)
        for c in range(width):
            weight_ref[c * rows : (c + 1) * rows, k * channels : (k + 1) * channels] = made[
                :, c * channels : (c + 1) * channels
            ]


def slopes_of(linear, scale, bias, upstream):
    return (
        upstream.astype(jnp.float32) * 2.0 * jnp.maximum(linear * scale + bias, 0.0)
    ).astype(jnp.bfloat16)


def regroup(chosen_ref, table_ref, width):
    count = chosen_ref.shape[0]
    rows = chosen_ref.shape[1] // width
    for c in range(width):
        table_ref[c * count : (c + 1) * count] = chosen_ref[:, c * rows : (c + 1) * rows]


def pull_back(slopes, decoder_ref, spread_ref, first, scale):
    count, _ = slopes[0].shape
    width = spread_ref.shape[1] // count
    back = lax.dot_general(
        decoder_ref[...], jnp.concatenate(slopes, axis=0), (((1,), (1,)), ((), ())),
        preferred_element_type=jnp.float32,
    )
    back = (back * scale).astype(jnp.bfloat16)
    for k in range(len(slopes)):
        at = (first + k) * width
        for c in range(width):
            spread_ref[at : at + width, c * count : (c + 1) * count] = back[
                c * width : (c + 1) * width, k * count : (k + 1) * count
            ]


def ahead_kernel(near_ref, far_low_ref, far_high_ref, pick_left_ref, pick_right_ref, mine_left_ref,
                 mine_right_ref, by_left_ref, by_right_ref, decoder_ref, bias_ref, up_ref,
                 out_ref, linear_ref, right_table_ref,
                 all_ref, chosen_ref, other_ref, weight_ref, left_table_ref, spread_ref):
    residues, width, rows = mine_left_ref.shape
    channels = bias_ref.shape[1]
    near = near_ref.shape[0]
    half = far_low_ref.shape[0]
    scale = 1.0 / rows
    all_ref[0:near] = near_ref[...]
    all_ref[near : near + half] = far_low_ref[...]
    all_ref[near + half :] = far_high_ref[...]
    chosen_ref[...] = jnp.dot(
        pick_left_ref[...], all_ref[...], preferred_element_type=jnp.float32
    ).astype(jnp.bfloat16)
    other_ref[...] = jnp.dot(
        pick_right_ref[...], all_ref[...], preferred_element_type=jnp.float32
    ).astype(jnp.bfloat16)
    regroup(chosen_ref, left_table_ref, width)
    regroup(other_ref, right_table_ref, width)
    bias = bias_ref[...]
    for first in range(0, residues, TOGETHER):
        build_weight(mine_right_ref, by_right_ref[...], weight_ref, first)
        linear = jnp.dot(chosen_ref[...], weight_ref[...], preferred_element_type=jnp.float32)
        slopes = [
            slopes_of(
                linear[:, k * channels : (k + 1) * channels], scale, bias,
                up_ref[:, (first + k) * channels : (first + k + 1) * channels],
            )
            for k in range(TOGETHER)
        ]
        pull_back(slopes, decoder_ref, spread_ref, first, scale)
        build_weight(mine_left_ref, by_left_ref[...], weight_ref, first)
        linear_ref[:, first * channels : (first + TOGETHER) * channels] = jnp.dot(
            other_ref[...], weight_ref[...], preferred_element_type=jnp.float32
        )
    out_ref[...] = jnp.dot(
        spread_ref[...], left_table_ref[...], preferred_element_type=jnp.float32
    )


def behind_kernel(linear_ref, right_table_ref, decoder_ref, bias_ref, up_ref, out_ref, spread_ref):
    channels = bias_ref.shape[1]
    rows = right_table_ref.shape[1]
    residues = linear_ref.shape[1] // channels
    scale = 1.0 / rows
    for first in range(0, residues, TOGETHER):
        slopes = []
        for k in range(TOGETHER):
            span = slice((first + k) * channels, (first + k + 1) * channels)
            slopes.append(slopes_of(linear_ref[:, span], scale, bias_ref[...], up_ref[:, span]))
        pull_back(slopes, decoder_ref, spread_ref, first, scale)
    out_ref[...] = jnp.dot(
        spread_ref[...], right_table_ref[...], preferred_element_type=jnp.float32
    )


def ahead_call(near, far_low, far_high, pick_left, pick_right, mine_left, mine_right, by_left,
               by_right, decoder, bias, up):
    residues, width, rows = mine_left.shape
    channels = bias.shape[1]
    count, wide = pick_left.shape
    return pl.pallas_call(
        ahead_kernel,
        out_shape=(
            jax.ShapeDtypeStruct((residues * width, rows), jnp.float32),
            jax.ShapeDtypeStruct((count, residues * channels), jnp.float32),
            jax.ShapeDtypeStruct((width * count, rows), jnp.bfloat16),
        ),
        scratch_shapes=[
            pltpu.VMEM((wide, width * rows), jnp.bfloat16),
            pltpu.VMEM((count, width * rows), jnp.bfloat16),
            pltpu.VMEM((count, width * rows), jnp.bfloat16),
            pltpu.VMEM((width * rows, TOGETHER * channels), jnp.bfloat16),
            pltpu.VMEM((width * count, rows), jnp.bfloat16),
            pltpu.VMEM((residues * width, width * count), jnp.bfloat16),
        ],
        compiler_params=pltpu.CompilerParams(vmem_limit_bytes=32 * 1024 * 1024),
        cost_estimate=pl.CostEstimate(
            flops=6_000_000_000, bytes_accessed=4_000_000, transcendentals=0
        ),
        interpret=INTERPRET,
        name="pair_ahead",
    )(near, far_low, far_high, pick_left, pick_right, mine_left, mine_right, by_left, by_right,
      decoder, bias, up)


def behind_call(linear, right_table, decoder, bias, up):
    count = linear.shape[0]
    width = right_table.shape[0] // count
    rows = right_table.shape[1]
    residues = linear.shape[1] // bias.shape[1]
    return pl.pallas_call(
        behind_kernel,
        out_shape=jax.ShapeDtypeStruct((residues * width, rows), jnp.float32),
        scratch_shapes=[pltpu.VMEM((residues * width, width * count), jnp.bfloat16)],
        compiler_params=pltpu.CompilerParams(vmem_limit_bytes=16 * 1024 * 1024),
        cost_estimate=pl.CostEstimate(
            flops=2_000_000_000, bytes_accessed=4_000_000, transcendentals=0
        ),
        interpret=INTERPRET,
        name="pair_behind",
    )(linear, right_table, decoder, bias, up)


def steps(
    homolog_embedding,
    left_factor_matrix,
    right_factor_matrix,
    decoder,
    pair_output_bias,
    pair_output_gradient,
):
    rows, local, _ = homolog_embedding.shape
    width = left_factor_matrix.shape[1]
    channels = decoder.shape[1]
    high = lax.axis_size("high")
    chips = high * 2
    core = lax.axis_index("core")
    low = lax.axis_index("low")
    z = ("high", "low")
    pair = 2 * local
    swap = [(0, 1), (1, 0)]
    up = [(k, (k + 1) % chips) for k in range(chips)]
    down = [(k, (k - 1) % chips) for k in range(chips)]

    factors = jnp.concatenate([left_factor_matrix, right_factor_matrix], axis=1)
    operands = jnp.einsum(
        "sje,ek->jks", homolog_embedding, factors, preferred_element_type=jnp.float32
    ).astype(jnp.bfloat16)
    sent = jnp.concatenate([operands[:, :width], operands[:, width:]], axis=0)
    near = lax.all_gather(sent.reshape(pair, width * rows), "high", axis=0, tiled=True)
    half = near.shape[0] // 2
    far_low = lax.ppermute(near[:half], z, up)
    far_high = lax.ppermute(near[half:], z, down)
    turned = lax.all_to_all(pair_output_gradient, z, 0, 0, tiled=True)

    def pick(offset):
        row = lax.broadcasted_iota(jnp.int32, (chips * local, chips * pair), 0)
        column = lax.broadcasted_iota(jnp.int32, (chips * local, chips * pair), 1)
        chip = row // local
        source = (chip // 2) * pair + offset * local + row % local
        source = source + jnp.where(chip % 2 == low, 0, high * pair)
        return (column == source).astype(jnp.bfloat16)

    operands, _ = lax.optimization_barrier((operands, near))
    partner = lax.ppermute(operands, "core", swap)
    mine_right = jnp.concatenate([operands[:, width:], partner[:, width:]], axis=0)
    mine_left = jnp.where(
        core == 0,
        jnp.concatenate([operands[:, :width], partner[:, :width]], axis=0),
        jnp.concatenate([partner[:, :width], operands[:, :width]], axis=0),
    )
    gradient = pair_output_gradient.reshape(chips, 2, local, local, channels)
    theirs = lax.ppermute(jnp.where(core == 0, gradient[:, 1], gradient[:, 0]), "core", swap)
    ours = jnp.where(core == 0, gradient[:, 0], gradient[:, 1])
    by_column = jnp.concatenate(
        [
            ours.reshape(chips, local, local * channels),
            theirs.reshape(chips, local, local * channels),
        ],
        axis=2,
    )
    by_column = by_column.reshape(chips * local, pair * channels)

    by_left = decoder.reshape(width, width * channels)
    by_right = (
        decoder.reshape(width, width, channels).transpose(1, 0, 2).reshape(width, width * channels)
    )
    bias = pair_output_bias.reshape(1, channels)
    second, linear, right_table = ahead_call(
        near, far_low, far_high, pick(0), pick(1), mine_left, mine_right, by_left, by_right,
        decoder, bias, by_column,
    )
    second = second.reshape(2, local, width, rows)
    second = second[0] + lax.ppermute(second[1], "core", swap)

    by_row = (
        turned.reshape(chips, pair, local, channels)
        .transpose(0, 2, 1, 3)
        .reshape(chips * local, pair * channels)
    )
    first = behind_call(
        linear, right_table, by_right.reshape(decoder.shape), bias, by_row
    )
    first = first.reshape(2, local, width, rows)
    first = jnp.where(core == 0, first[0], first[1]) + lax.ppermute(
        jnp.where(core == 0, first[1], first[0]), "core", swap
    )
    alignment = jnp.einsum(
        "jks,ek->sje",
        jnp.concatenate([first, second], axis=1).astype(jnp.bfloat16),
        factors,
        preferred_element_type=jnp.float32,
    ).astype(jnp.bfloat16)
    return first.transpose(2, 0, 1), second.transpose(2, 0, 1), alignment


def solution(mesh):
    groups = mesh.shape["group"]
    split = Mesh(
        mesh.devices.reshape(groups, mesh.shape["col"] // 4, 2, 2), ("group", "high", "low", "core")
    )
    tall = P("group", ("high", "low", "core"), None)
    return jax.shard_map(
        steps,
        mesh=split,
        in_specs=(tall, P(), P(), P(), P(), tall),
        out_specs=(tall, tall, tall),
        check_vma=False,
    )
```

time: 136 us -> 127 us (0.934)
  Pallas kernels: 18.1 us -> 10.4 us
  waiting for transfers between devices: 28.5 us -> 26.5 us
    pallas_call x1, Pallas kernels: 13.8 us -> 9.09 us  [ahead_call(): pl.pallas_call(ahead_kernel, out_shape=(jax.ShapeDtypeStruct((residues *...]
    pallas_call x1, Pallas kernels: 4.31 us -> 1.32 us  [behind_call(): pl.pallas_call(behind_kernel, out_shape=jax.ShapeDtypeStruct((residues *...]
    ppermute x1, waiting for transfers between devices: 28.3 us -> 26 us  [steps(): far_low = lax.ppermute(near[:half], z, up)]
    unnamed x18 -> x19, local copies, waits for them, and re-layouts: 4.1 us -> 6.27 us
  transfers between devices with their start and end apart: 7 -> 7, of which waited for: 2 -> 2; matrix products, arithmetic and copies ran while one was open for 3% -> 3% of each run, Pallas kernels for 13% -> 8%
where the time goes in v1:
time: 127 us; the launch traced here: 125 us
  blocking collectives  60.9 us (48%)
  waiting for transfers between devices  26.5 us (21%)
  starting transfers between devices  15.2 us (12%)
  Pallas kernels  10.4 us (8%)
  local copies, waits for them, and re-layouts  7.64 us (6%)
  other arithmetic  2.66 us (2%)
    all_gather x1, blocking collectives, steps(): lax.all_gather(sent.reshape(pair, width * rows), 'high', axis=0, tiled=True)  60.9 us
    ppermute x1, waiting for transfers between devices, steps(): far_low = lax.ppermute(near[:half], z, up)  26 us
    all_to_all x1, starting transfers between devices, steps(): turned = lax.all_to_all(pair_output_gradient, z, 0, 0, tiled=True)  11.3 us
    pallas_call x1, Pallas kernels, ahead_call(): pl.pallas_call(ahead_kernel, out_shape=(jax.ShapeDtypeStruct((residues *...  9.09 us
    unnamed x19, local copies, waits for them, and re-layouts  6.27 us
  transfers between devices with their start and end apart: 7, of which 2 were waited for; matrix products, arithmetic and copies ran while one was open for 3% of the time, Pallas kernels for 8%

profile of v1, /device:TPU:38, one launch (start us, length us, event | category | flops | bytes accessed | tf_op | source)
XLA Modules:
  0.0 125.4 jit_solution(17177048528915035664)
XLA Ops:
  0.6 0.0 copy-start
  0.6 0.9 copy-done
  1.6 0.9 fusion.1
  2.5 0.1 reshape.58
  2.7 60.9 %all_gather.3.near_ref = bf16[128,3072]{1,0:T(8,128)(2,1)S(1)} all-gather(bf16[8,3072]{1,0:T(8,128)(2,1)S(1)} %reshape.58), channel_id=1, replica_groups=mesh['group'=4,'high'=16,'low'=2,'core'=2] {'high'}, dimensions={0}, use_global_device_ids=true | all-gather | bytes 835584 | tf_op jit(solution)/shard_map/all_gather | solution.py:188
  63.6 0.0 collective-permute-start.2
  63.6 11.3 %all-to-all-start = ((bf16[256,4,128]{2,1,0:T(4,128)(2,1)}), bf16[256,4,128]{2,1,0:T(4,128)(2,1)S(1)}, u32[]{:S(2)}, u32[]{:S(2)}) async-start(bf16[256,4,128]{2,1,0:T(4,128)(2,1)} %param.11), calls=%async_computation | async-start | bytes 524288 | tf_op jit(solution)/shard_map/all_to_all | solution.py:192
  74.9 1.1 broadcast_select_fusion
  76.0 0.3 collective-permute-start.3
  76.4 0.9 fusion.19
  77.3 1.1 collective-permute-start
  78.4 2.2 %collective-permute-start.1 = (bf16[64,3072]{1,0:T(8,128)(2,1)}, bf16[64,3072]{1,0:T(8,128)(2,1)S(1)}, u32[]{:S(2)}, u32[]{:S(2)}) collective-permute-start(bf16[64,3072]{1,0:T(8,128)(2,1)} %get-tuple-element.14), channel_id=1, source_target_pairs={{0,62},{2,0},{4,2},{6,4},{8,6},{10,8},{12,10},{14,12},{16,14},{18,... | collective-permute-start | bytes 1179656 | tf_op jit(solution)/shard_map/ppermute | solution.py:191
  80.6 0.0 copy-start.1
  80.6 0.2 fusion.11
  80.8 0.7 copy-done.1
  81.5 0.1 reshape.59.by_left_ref
  81.6 0.1 copy.10
  81.8 0.1 copy.28
  81.9 0.0 collective-permute-done.2
  81.9 0.0 collective-permute-done.3
  82.0 0.9 copy.29
  82.9 26.0 %collective-permute-done.far_low_ref = bf16[64,3072]{1,0:T(8,128)(2,1)S(1)} collective-permute-done((bf16[64,3072]{1,0:T(8,128)(2,1)}, bf16[64,3072]{1,0:T(8,128)(2,1)S(1)}, u32[]{:S(2)}, u32[]{:S(2)}) %collective-permute-start) | collective-permute-done | bytes 393248 | tf_op jit(solution)/shard_map/ppermute | solution.py:190
  108.9 0.0 collective-permute-done.1.far_high_ref
  108.9 0.0 copy-start.2
  108.9 0.7 copy-done.2
  109.5 9.1 %pair_ahead.1 = (f32[256,96]{1,0:T(8,128)S(1)}, f32[128,1024]{1,0:T(8,128)S(1)}, bf16[4096,96]{1,0:T(8,128)(2,1)S(1)}) custom-call(bf16[128,3072]{1,0:T(8,128)(2,1)S(1)} %all_gather.3.near_ref, bf16[64,3072]{1,0:T(8,128)(2,1)S(1)} %collective-permute-done.far_low_ref, bf16[64,3072]{1,0:T(8,128)(2,1)S(1)} %collective-permute-done.1.far_high_ref, ...), custom_call_target="tpu_custom_call" | custom-call | flops 6000000000 | bytes 4000000 | tf_op jit(solution)/shard_map/pair_ahead/pallas_call | solution.py:119
  118.6 0.0 copy-start.3
  118.6 1.0 copy-done.3
  119.6 0.0 copy-start.4
  119.7 0.1 collective-permute-start.5
  119.8 0.0 all-to-all-done
  119.9 0.9 copy-done.4
  120.9 1.3 %pair_behind.1 = f32[256,96]{1,0:T(8,128)S(1)} custom-call(f32[128,1024]{1,0:T(8,128)S(1)} %get-tuple-element.8.linear_ref, bf16[4096,96]{1,0:T(8,128)(2,1)S(1)} %copy-done.4, bf16[1024,128]{1,0:T(8,128)(2,1)S(1)} %bitcast.61, f32[1,128]{1,0:T(1,128)S(1)} %bitcast.65, bf16[128,1024]{1,0:T(8,128)(2,1)S(1)} %bitcast.63), custom_call_target="tpu_custom_call" | custom-call | flops 2000000000 | bytes 4000000 | tf_op jit(solution)/shard_map/pair_behind/pallas_call | solution.py:149
  122.2 0.1 collective-permute-start.4
  122.4 0.0 collective-permute-done.5
  122.4 0.6 add_convert_fusion
  123.0 0.6 collective-permute-done.4
  123.6 0.0 copy-start.5
  123.6 0.0 copy-start.6
  123.6 0.6 add_convert_fusion.1
  124.2 0.1 copy-done.5
  124.3 0.0 copy-done.6
  124.3 0.2 fusion
  124.6 0.8 copy.14
  (15 shorter events, 0.2 us)
Async XLA Ops:
  0.6 0.9 copy-start
  63.6 18.3 %collective-permute-start.2 = (bf16[4,64,96]{2,1,0:T(8,128)(2,1)S(1)}, bf16[4,64,96]{2,1,0:T(8,128)(2,1)S(1)}, u32[]{:S(2)}, u32[]{:S(2)}) collective-permute-start(bf16[4,64,96]{2,1,0:T(8,128)(2,1)S(1)} %fusion.1), channel_id=1, source_target_pairs={{0,1},{1,0},{2,3},{3,2},{4,5},{5,4},{6,7},{7,6},{8,9},{9,8},{10,11... | collective-permute-start | bytes 147464 | tf_op jit(solution)/shard_map/ppermute | solution.py:203
  63.6 56.2 %all-to-all-start = ((bf16[256,4,128]{2,1,0:T(4,128)(2,1)}), bf16[256,4,128]{2,1,0:T(4,128)(2,1)S(1)}, u32[]{:S(2)}, u32[]{:S(2)}) async-start(bf16[256,4,128]{2,1,0:T(4,128)(2,1)} %param.11), calls=%async_computation | async-start | bytes 524288 | tf_op jit(solution)/shard_map/all_to_all | solution.py:192
  76.0 5.9 %collective-permute-start.3 = (bf16[32,4,4,128]{3,2,1,0:T(4,128)(2,1)S(1)}, bf16[32,4,4,128]{3,2,1,0:T(4,128)(2,1)}, u32[]{:S(2)}, u32[]{:S(2)}) collective-permute-start(bf16[32,4,4,128]{3,2,1,0:T(4,128)(2,1)S(1)} %get-tuple-element.17), channel_id=1, source_target_pairs={{0,1},{1,0},{2,3},{3,2},{4,5},{5,4},{6,7},{7,6},{8,9},{9,8},{10,11... | collective-permute-start | bytes 393224 | tf_op jit(solution)/shard_map/ppermute | solution.py:211
  77.3 31.6 %collective-permute-start = (bf16[64,3072]{1,0:T(8,128)(2,1)}, bf16[64,3072]{1,0:T(8,128)(2,1)S(1)}, u32[]{:S(2)}, u32[]{:S(2)}) collective-permute-start(bf16[64,3072]{1,0:T(8,128)(2,1)} %get-tuple-element.15), channel_id=1, source_target_pairs={{0,2},{2,4},{4,6},{6,8},{8,10},{10,12},{12,14},{14,16},{16,18},{18... | collective-permute-start | bytes 1179656 | tf_op jit(solution)/shard_map/ppermute | solution.py:190
  78.4 30.5 %collective-permute-start.1 = (bf16[64,3072]{1,0:T(8,128)(2,1)}, bf16[64,3072]{1,0:T(8,128)(2,1)S(1)}, u32[]{:S(2)}, u32[]{:S(2)}) collective-permute-start(bf16[64,3072]{1,0:T(8,128)(2,1)} %get-tuple-element.14), channel_id=1, source_target_pairs={{0,62},{2,0},{4,2},{6,4},{8,6},{10,8},{12,10},{14,12},{16,14},{18,... | collective-permute-start | bytes 1179656 | tf_op jit(solution)/shard_map/ppermute | solution.py:191
  80.6 1.0 copy-start.1
  108.9 0.7 copy-start.2
  118.6 1.0 copy-start.3
  119.6 1.2 copy-start.4
  119.7 2.7 %collective-permute-start.5 = (f32[4,32,96]{2,1,0:T(8,128)S(1)}, f32[4,32,96]{2,1,0:T(8,128)S(1)}, u32[]{:S(2)}, u32[]{:S(2)}) collective-permute-start(f32[4,32,96]{2,1,0:T(8,128)S(1)} %bitcast.73), channel_id=1, source_target_pairs={{0,1},{1,0},{2,3},{3,2},{4,5},{5,4},{6,7},{7,6},{8,9},{9,8},{10,11... | collective-permute-start | bytes 147464 | tf_op jit(solution)/shard_map/ppermute | solution.py:232
  122.2 1.4 %collective-permute-start.4 = (f32[4,32,96]{2,1,0:T(8,128)S(1)}, f32[4,32,96]{2,1,0:T(8,128)S(1)}, u32[]{:S(2)}, u32[]{:S(2)}) collective-permute-start(f32[4,32,96]{2,1,0:T(8,128)S(1)} %bitcast.74), channel_id=1, source_target_pairs={{0,1},{1,0},{2,3},{3,2},{4,5},{5,4},{6,7},{7,6},{8,9},{9,8},{10,11... | collective-permute-start | bytes 147464 | tf_op jit(solution)/shard_map/ppermute | solution.py:243
  123.6 0.7 copy-start.5
  123.6 0.7 copy-start.6

commit v2 on v1

--- a/solution.py
+++ b/solution.py
@@ -11,24 +11,27 @@
 TOGETHER = 2
 
 
-def build_weight(mine_ref, mix, weight_ref, first):
-    _, width, rows = mine_ref.shape
-    channels = mix.shape[1] // width
-    for k in range(TOGETHER):
-        made = lax.dot_general(
-            mine_ref[first + k], mix, (((0,), (0,)), ((), ())),
-            preferred_element_type=jnp.float32,
-        ).astype(jnp.bfloat16)
+def slopes_of(linear, bias, upstream):
+    return (upstream.astype(jnp.float32) * 2.0 * jnp.maximum(linear + bias, 0.0)).astype(
+        jnp.bfloat16
+    )
+
+
+def push_forward(mine, table_ref, decoder_ref, spread_ref, width, scale):
+    count = table_ref.shape[0] // width
+    made = lax.dot_general(
+        mine, table_ref[...], (((1,), (1,)), ((), ())), preferred_element_type=jnp.float32
+    )
+    made = (made * scale).astype(jnp.bfloat16)
+    for k in range(mine.shape[0] // width):
         for c in range(width):
-            weight_ref[c * rows : (c + 1) * rows, k * channels : (k + 1) * channels] = made[
-                :, c * channels : (c + 1) * channels
+            spread_ref[c * width : (c + 1) * width, k * count : (k + 1) * count] = made[
+                k * width : (k + 1) * width, c * count : (c + 1) * count
             ]
-
-
-def slopes_of(linear, scale, bias, upstream):
-    return (
-        upstream.astype(jnp.float32) * 2.0 * jnp.maximum(linear * scale + bias, 0.0)
-    ).astype(jnp.bfloat16)
+    return lax.dot_general(
+        decoder_ref[...], spread_ref[...], (((0,), (0,)), ((), ())),
+        preferred_element_type=jnp.float32,
+    )
 
 
 def regroup(chosen_ref, table_ref, width):
@@ -55,44 +58,45 @@
 
 
 def ahead_kernel(near_ref, far_low_ref, far_high_ref, pick_left_ref, pick_right_ref, mine_left_ref,
-                 mine_right_ref, by_left_ref, by_right_ref, decoder_ref, bias_ref, up_ref,
+                 mine_right_ref, decoder_ref, turned_decoder_ref, bias_ref, up_ref,
                  out_ref, linear_ref, right_table_ref,
-                 all_ref, chosen_ref, other_ref, weight_ref, left_table_ref, spread_ref):
+                 all_ref, chosen_ref, left_table_ref, product_ref, spread_ref):
     residues, width, rows = mine_left_ref.shape
     channels = bias_ref.shape[1]
+    count = up_ref.shape[0]
     near = near_ref.shape[0]
     half = far_low_ref.shape[0]
     scale = 1.0 / rows
     all_ref[0:near] = near_ref[...]
     all_ref[near : near + half] = far_low_ref[...]
     all_ref[near + half :] = far_high_ref[...]
-    chosen_ref[...] = jnp.dot(
-        pick_left_ref[...], all_ref[...], preferred_element_type=jnp.float32
-    ).astype(jnp.bfloat16)
-    other_ref[...] = jnp.dot(
-        pick_right_ref[...], all_ref[...], preferred_element_type=jnp.float32
-    ).astype(jnp.bfloat16)
-    regroup(chosen_ref, left_table_ref, width)
-    regroup(other_ref, right_table_ref, width)
-    bias = bias_ref[...]
+    for pick_ref, table_ref in ((pick_left_ref, left_table_ref), (pick_right_ref, right_table_ref)):
+        chosen_ref[...] = jnp.dot(
+            pick_ref[...], all_ref[...], preferred_element_type=jnp.float32
+        ).astype(jnp.bfloat16)
+        regroup(chosen_ref, table_ref, width)
+    linear = push_forward(
+        mine_right_ref[...].reshape(residues * width, rows), left_table_ref, decoder_ref,
+        product_ref, width, scale,
+    )
     for first in range(0, residues, TOGETHER):
-        build_weight(mine_right_ref, by_right_ref[...], weight_ref, first)
-        linear = jnp.dot(chosen_ref[...], weight_ref[...], preferred_element_type=jnp.float32)
         slopes = [
             slopes_of(
-                linear[:, k * channels : (k + 1) * channels], scale, bias,
-                up_ref[:, (first + k) * channels : (first + k + 1) * channels],
+                linear[:, k * count : (k + 1) * count].T, bias_ref[...],
+                up_ref[:, k * channels : (k + 1) * channels],
             )
-            for k in range(TOGETHER)
+            for k in range(first, first + TOGETHER)
         ]
         pull_back(slopes, decoder_ref, spread_ref, first, scale)
-        build_weight(mine_left_ref, by_left_ref[...], weight_ref, first)
-        linear_ref[:, first * channels : (first + TOGETHER) * channels] = jnp.dot(
-            other_ref[...], weight_ref[...], preferred_element_type=jnp.float32
-        )
     out_ref[...] = jnp.dot(
         spread_ref[...], left_table_ref[...], preferred_element_type=jnp.float32
     )
+    linear = push_forward(
+        mine_left_ref[...].reshape(residues * width, rows), right_table_ref, turned_decoder_ref,
+        product_ref, width, scale,
+    )
+    for k in range(residues):
+        linear_ref[:, k * channels : (k + 1) * channels] = linear[:, k * count : (k + 1) * count].T
 
 
 def behind_kernel(linear_ref, right_table_ref, decoder_ref, bias_ref, up_ref, out_ref, spread_ref):
@@ -104,15 +108,15 @@
         slopes = []
         for k in range(TOGETHER):
             span = slice((first + k) * channels, (first + k + 1) * channels)
-            slopes.append(slopes_of(linear_ref[:, span], scale, bias_ref[...], up_ref[:, span]))
+            slopes.append(slopes_of(linear_ref[:, span], bias_ref[...], up_ref[:, span]))
         pull_back(slopes, decoder_ref, spread_ref, first, scale)
     out_ref[...] = jnp.dot(
         spread_ref[...], right_table_ref[...], preferred_element_type=jnp.float32
     )
 
 
-def ahead_call(near, far_low, far_high, pick_left, pick_right, mine_left, mine_right, by_left,
-               by_right, decoder, bias, up):
+def ahead_call(near, far_low, far_high, pick_left, pick_right, mine_left, mine_right, decoder,
+               turned_decoder, bias, up):
     residues, width, rows = mine_left.shape
     channels = bias.shape[1]
     count, wide = pick_left.shape
@@ -126,19 +130,18 @@
         scratch_shapes=[
             pltpu.VMEM((wide, width * rows), jnp.bfloat16),
             pltpu.VMEM((count, width * rows), jnp.bfloat16),
-            pltpu.VMEM((count, width * rows), jnp.bfloat16),
-            pltpu.VMEM((width * rows, TOGETHER * channels), jnp.bfloat16),
             pltpu.VMEM((width * count, rows), jnp.bfloat16),
+            pltpu.VMEM((width * width, residues * count), jnp.bfloat16),
             pltpu.VMEM((residues * width, width * count), jnp.bfloat16),
         ],
         compiler_params=pltpu.CompilerParams(vmem_limit_bytes=32 * 1024 * 1024),
         cost_estimate=pl.CostEstimate(
-            flops=6_000_000_000, bytes_accessed=4_000_000, transcendentals=0
+            flops=3_000_000_000, bytes_accessed=4_000_000, transcendentals=0
         ),
         interpret=INTERPRET,
         name="pair_ahead",
-    )(near, far_low, far_high, pick_left, pick_right, mine_left, mine_right, by_left, by_right,
-      decoder, bias, up)
+    )(near, far_low, far_high, pick_left, pick_right, mine_left, mine_right, decoder,
+      turned_decoder, bias, up)
 
 
 def behind_call(linear, right_table, decoder, bias, up):
@@ -219,14 +222,13 @@
     )
     by_column = by_column.reshape(chips * local, pair * channels)
 
-    by_left = decoder.reshape(width, width * channels)
-    by_right = (
-        decoder.reshape(width, width, channels).transpose(1, 0, 2).reshape(width, width * channels)
+    turned_decoder = (
+        decoder.reshape(width, width, channels).transpose(1, 0, 2).reshape(decoder.shape)
     )
     bias = pair_output_bias.reshape(1, channels)
     second, linear, right_table = ahead_call(
-        near, far_low, far_high, pick(0), pick(1), mine_left, mine_right, by_left, by_right,
-        decoder, bias, by_column,
+        near, far_low, far_high, pick(0), pick(1), mine_left, mine_right, decoder,
+        turned_decoder, bias, by_column,
     )
     second = second.reshape(2, local, width, rows)
     second = second[0] + lax.ppermute(second[1], "core", swap)
@@ -237,7 +239,7 @@
         .reshape(chips * local, pair * channels)
     )
     first = behind_call(
-        linear, right_table, by_right.reshape(decoder.shape), bias, by_row
+        linear, right_table, turned_decoder, bias, by_row
     )
     first = first.reshape(2, local, width, rows)
     first = jnp.where(core == 0, first[0], first[1]) + lax.ppermute(

time: 127 us -> 125 us (0.984)
  waiting for transfers between devices: 26.5 us -> 31.7 us
  Pallas kernels: 10.4 us -> 5.22 us
  local copies, waits for them, and re-layouts: 7.64 us -> 5.42 us
    pallas_call x1, Pallas kernels: 9.09 us -> 3.88 us  [ahead_call(): pl.pallas_call(ahead_kernel, out_shape=(jax.ShapeDtypeStruct((residues *...]
    all_to_all x1, waiting for transfers between devices: 0.01 us -> 3.25 us  [steps(): turned = lax.all_to_all(pair_output_gradient, z, 0, 0, tiled=True)]
    ppermute x1, waiting for transfers between devices: 26 us -> 27.9 us  [steps(): far_low = lax.ppermute(near[:half], z, up)]
    unnamed x19 -> x18, local copies, waits for them, and re-layouts: 6.27 us -> 5.06 us
  transfers between devices with their start and end apart: 7 -> 7, of which waited for: 2 -> 3; matrix products, arithmetic and copies ran while one was open for 3% -> 2% of each run, Pallas kernels for 8% -> 4%
where the time goes in v2:
time: 125 us; the launch traced here: 123 us
  blocking collectives  60.9 us (49%)
  waiting for transfers between devices  31.7 us (25%)
  starting transfers between devices  15.3 us (12%)
  local copies, waits for them, and re-layouts  5.42 us (4%)
  Pallas kernels  5.22 us (4%)
  other arithmetic  2.66 us (2%)
    all_gather x1, blocking collectives, steps(): lax.all_gather(sent.reshape(pair, width * rows), 'high', axis=0, tiled=True)  60.9 us
    ppermute x1, waiting for transfers between devices, steps(): far_low = lax.ppermute(near[:half], z, up)  27.9 us
    all_to_all x1, starting transfers between devices, steps(): turned = lax.all_to_all(pair_output_gradient, z, 0, 0, tiled=True)  11.3 us
    unnamed x18, local copies, waits for them, and re-layouts  5.06 us
    pallas_call x1, Pallas kernels, ahead_call(): pl.pallas_call(ahead_kernel, out_shape=(jax.ShapeDtypeStruct((residues *...  3.88 us
    all_to_all x1, waiting for transfers between devices, steps(): turned = lax.all_to_all(pair_output_gradient, z, 0, 0, tiled=True)  3.25 us
  transfers between devices with their start and end apart: 7, of which 3 were waited for; matrix products, arithmetic and copies ran while one was open for 2% of the time, Pallas kernels for 4%

profile of v2, /device:TPU:38, one launch (start us, length us, event | category | flops | bytes accessed | tf_op | source)
XLA Modules:
  0.0 123.2 jit_solution(5816509203670324025)
XLA Ops:
  0.6 0.0 copy-start
  0.6 0.9 copy-done
  1.6 0.9 fusion.1
  2.5 0.1 reshape.55
  2.7 60.9 %all_gather.3.near_ref = bf16[128,3072]{1,0:T(8,128)(2,1)S(1)} all-gather(bf16[8,3072]{1,0:T(8,128)(2,1)S(1)} %reshape.55), channel_id=1, replica_groups=mesh['group'=4,'high'=16,'low'=2,'core'=2] {'high'}, dimensions={0}, use_global_device_ids=true | all-gather | bytes 835584 | tf_op jit(solution)/shard_map/all_gather | solution.py:191
  63.6 0.0 collective-permute-start.2
  63.6 11.3 %all-to-all-start = ((bf16[256,4,128]{2,1,0:T(4,128)(2,1)}), bf16[256,4,128]{2,1,0:T(4,128)(2,1)S(1)}, u32[]{:S(2)}, u32[]{:S(2)}) async-start(bf16[256,4,128]{2,1,0:T(4,128)(2,1)} %param.11), calls=%async_computation | async-start | bytes 524288 | tf_op jit(solution)/shard_map/all_to_all | solution.py:195
  74.9 1.1 broadcast_select_fusion
  76.0 0.3 collective-permute-start.3
  76.4 0.1 fusion.19
  76.4 1.2 collective-permute-start
  77.6 2.2 %collective-permute-start.1 = (bf16[64,3072]{1,0:T(8,128)(2,1)S(1)}, bf16[64,3072]{1,0:T(8,128)(2,1)S(1)}, u32[]{:S(2)}, u32[]{:S(2)}) collective-permute-start(bf16[64,3072]{1,0:T(8,128)(2,1)S(1)} %get-tuple-element.14), channel_id=1, source_target_pairs={{0,62},{2,0},{4,2},{6,4},{8,6},{10,8},{12,10},{14,12},{16,14},{18,... | collective-permute-start | bytes 1179656 | tf_op jit(solution)/shard_map/ppermute | solution.py:194
  79.8 0.0 copy-start.1
  79.8 0.2 fusion.11
  80.0 0.7 copy-done.1
  80.7 0.1 copy.10
  80.9 0.0 collective-permute-done.2
  80.9 0.0 collective-permute-done.3
  81.0 27.9 %collective-permute-done.far_low_ref = bf16[64,3072]{1,0:T(8,128)(2,1)S(1)} collective-permute-done((bf16[64,3072]{1,0:T(8,128)(2,1)S(1)}, bf16[64,3072]{1,0:T(8,128)(2,1)S(1)}, u32[]{:S(2)}, u32[]{:S(2)}) %collective-permute-start) | collective-permute-done | bytes 393248 | tf_op jit(solution)/shard_map/ppermute | solution.py:193
  108.9 0.0 collective-permute-done.1.far_high_ref
  108.9 0.0 copy-start.2
  108.9 0.7 copy-done.2
  109.5 3.9 %pair_ahead.1 = (f32[256,96]{1,0:T(8,128)S(1)}, f32[128,1024]{1,0:T(8,128)S(1)}, bf16[4096,96]{1,0:T(8,128)(2,1)S(1)}) custom-call(bf16[128,3072]{1,0:T(8,128)(2,1)S(1)} %all_gather.3.near_ref, bf16[64,3072]{1,0:T(8,128)(2,1)S(1)} %collective-permute-done.far_low_ref, bf16[64,3072]{1,0:T(8,128)(2,1)S(1)} %collective-permute-done.1.far_high_ref, ...), custom_call_target="tpu_custom_call" | custom-call | flops 3000000000 | bytes 4000000 | tf_op jit(solution)/shard_map/pair_ahead/pallas_call | solution.py:123
  113.4 0.0 copy-start.3
  113.4 0.8 copy-done.3
  114.2 0.1 collective-permute-start.5
  114.4 3.2 %all-to-all-done = bf16[256,4,128]{2,1,0:T(4,128)(2,1)S(1)} async-done(((bf16[256,4,128]{2,1,0:T(4,128)(2,1)}), bf16[256,4,128]{2,1,0:T(4,128)(2,1)S(1)}, u32[]{:S(2)}, u32[]{:S(2)}) %all-to-all-start) | async-done | bytes 262176 | tf_op jit(solution)/shard_map/all_to_all | solution.py:195
  117.6 0.0 copy-start.4
  117.7 0.9 copy-done.4
  118.7 1.3 %pair_behind.1 = f32[256,96]{1,0:T(8,128)S(1)} custom-call(f32[128,1024]{1,0:T(8,128)S(1)} %copy-done.4, bf16[4096,96]{1,0:T(8,128)(2,1)S(1)} %get-tuple-element.9.right_table_ref, bf16[1024,128]{1,0:T(8,128)(2,1)S(1)} %bitcast.57, f32[1,128]{1,0:T(1,128)S(1)} %bitcast.60, bf16[128,1024]{1,0:T(8,128)(2,1)S(1)} %bitcast.58), custom_call_target="tpu_custom_call" | custom-call | flops 2000000000 | bytes 4000000 | tf_op jit(solution)/shard_map/pair_behind/pallas_call | solution.py:152
  120.0 0.1 collective-permute-start.4
  120.2 0.0 collective-permute-done.5
  120.2 0.6 add_convert_fusion
  120.9 0.6 collective-permute-done.4
  121.4 0.0 copy-start.5
  121.4 0.0 copy-start.6
  121.4 0.6 add_convert_fusion.1
  122.1 0.1 copy-done.5
  122.1 0.0 copy-done.6
  122.2 0.2 fusion
  122.4 0.8 copy.14
  (16 shorter events, 0.3 us)
Async XLA Ops:
  0.6 0.9 copy-start
  63.6 17.3 %collective-permute-start.2 = (bf16[4,64,96]{2,1,0:T(8,128)(2,1)S(1)}, bf16[4,64,96]{2,1,0:T(8,128)(2,1)S(1)}, u32[]{:S(2)}, u32[]{:S(2)}) collective-permute-start(bf16[4,64,96]{2,1,0:T(8,128)(2,1)S(1)} %fusion.1), channel_id=1, source_target_pairs={{0,1},{1,0},{2,3},{3,2},{4,5},{5,4},{6,7},{7,6},{8,9},{9,8},{10,11... | collective-permute-start | bytes 147464 | tf_op jit(solution)/shard_map/ppermute | solution.py:206
  63.6 54.0 %all-to-all-start = ((bf16[256,4,128]{2,1,0:T(4,128)(2,1)}), bf16[256,4,128]{2,1,0:T(4,128)(2,1)S(1)}, u32[]{:S(2)}, u32[]{:S(2)}) async-start(bf16[256,4,128]{2,1,0:T(4,128)(2,1)} %param.11), calls=%async_computation | async-start | bytes 524288 | tf_op jit(solution)/shard_map/all_to_all | solution.py:195
  76.0 4.9 %collective-permute-start.3 = (bf16[32,4,4,128]{3,2,1,0:T(4,128)(2,1)S(1)}, bf16[32,4,4,128]{3,2,1,0:T(4,128)(2,1)S(1)}, u32[]{:S(2)}, u32[]{:S(2)}) collective-permute-start(bf16[32,4,4,128]{3,2,1,0:T(4,128)(2,1)S(1)} %get-tuple-element.17), channel_id=1, source_target_pairs={{0,1},{1,0},{2,3},{3,2},{4,5},{5,4},{6,7},{7,6},{8,9},{9,8},{10,11... | collective-permute-start | bytes 393224 | tf_op jit(solution)/shard_map/ppermute | solution.py:214
  76.4 32.5 %collective-permute-start = (bf16[64,3072]{1,0:T(8,128)(2,1)S(1)}, bf16[64,3072]{1,0:T(8,128)(2,1)S(1)}, u32[]{:S(2)}, u32[]{:S(2)}) collective-permute-start(bf16[64,3072]{1,0:T(8,128)(2,1)S(1)} %get-tuple-element.15), channel_id=1, source_target_pairs={{0,2},{2,4},{4,6},{6,8},{8,10},{10,12},{12,14},{14,16},{16,18},{18... | collective-permute-start | bytes 1179656 | tf_op jit(solution)/shard_map/ppermute | solution.py:193
  77.6 31.3 %collective-permute-start.1 = (bf16[64,3072]{1,0:T(8,128)(2,1)S(1)}, bf16[64,3072]{1,0:T(8,128)(2,1)S(1)}, u32[]{:S(2)}, u32[]{:S(2)}) collective-permute-start(bf16[64,3072]{1,0:T(8,128)(2,1)S(1)} %get-tuple-element.14), channel_id=1, source_target_pairs={{0,62},{2,0},{4,2},{6,4},{8,6},{10,8},{12,10},{14,12},{16,14},{18,... | collective-permute-start | bytes 1179656 | tf_op jit(solution)/shard_map/ppermute | solution.py:194
  79.8 1.0 copy-start.1
  108.9 0.7 copy-start.2
  113.4 0.8 copy-start.3
  114.2 6.0 %collective-permute-start.5 = (f32[4,32,96]{2,1,0:T(8,128)S(1)}, f32[4,32,96]{2,1,0:T(8,128)S(1)}, u32[]{:S(2)}, u32[]{:S(2)}) collective-permute-start(f32[4,32,96]{2,1,0:T(8,128)S(1)} %bitcast.69), channel_id=1, source_target_pairs={{0,1},{1,0},{2,3},{3,2},{4,5},{5,4},{6,7},{7,6},{8,9},{9,8},{10,11... | collective-permute-start | bytes 147464 | tf_op jit(solution)/shard_map/ppermute | solution.py:234
  117.6 1.0 copy-start.4
  120.0 1.4 %collective-permute-start.4 = (f32[4,32,96]{2,1,0:T(8,128)S(1)}, f32[4,32,96]{2,1,0:T(8,128)S(1)}, u32[]{:S(2)}, u32[]{:S(2)}) collective-permute-start(f32[4,32,96]{2,1,0:T(8,128)S(1)} %bitcast.70), channel_id=1, source_target_pairs={{0,1},{1,0},{2,3},{3,2},{4,5},{5,4},{6,7},{7,6},{8,9},{9,8},{10,11... | collective-permute-start | bytes 147464 | tf_op jit(solution)/shard_map/ppermute | solution.py:245
  121.4 0.7 copy-start.5
  121.4 0.7 copy-start.6

commit v3 on v2

--- a/solution.py
+++ b/solution.py
@@ -108,7 +108,10 @@
         slopes = []
         for k in range(TOGETHER):
             span = slice((first + k) * channels, (first + k + 1) * channels)
-            slopes.append(slopes_of(linear_ref[:, span], bias_ref[...], up_ref[:, span]))
+            slopes.append(slopes_of(
+                linear_ref[:, span], bias_ref[...],
+                up_ref[:, first + k].reshape(linear_ref.shape[0], channels),
+            ))
         pull_back(slopes, decoder_ref, spread_ref, first, scale)
     out_ref[...] = jnp.dot(
         spread_ref[...], right_table_ref[...], preferred_element_type=jnp.float32
@@ -230,21 +233,20 @@
         near, far_low, far_high, pick(0), pick(1), mine_left, mine_right, decoder,
         turned_decoder, bias, by_column,
     )
-    second = second.reshape(2, local, width, rows)
-    second = second[0] + lax.ppermute(second[1], "core", swap)
-
-    by_row = (
-        turned.reshape(chips, pair, local, channels)
-        .transpose(0, 2, 1, 3)
-        .reshape(chips * local, pair * channels)
-    )
+    by_row = turned.reshape(chips, pair, local, channels)
     first = behind_call(
         linear, right_table, turned_decoder, bias, by_row
     )
+    first, second = lax.optimization_barrier((first, second))
     first = first.reshape(2, local, width, rows)
-    first = jnp.where(core == 0, first[0], first[1]) + lax.ppermute(
-        jnp.where(core == 0, first[1], first[0]), "core", swap
-    )
+    second = second.reshape(2, local, width, rows)
+    got = lax.ppermute(
+        jnp.concatenate([jnp.where(core == 0, first[1], first[0]), second[1]], axis=0),
+        "core",
+        swap,
+    )
+    first = jnp.where(core == 0, first[0], first[1]) + got[:local]
+    second = second[0] + got[local:]
     alignment = jnp.einsum(
         "jks,ek->sje",
         jnp.concatenate([first, second], axis=1).astype(jnp.bfloat16),

time: 125 us -> 125 us (level)
    unnamed x18 -> x17, local copies, waits for them, and re-layouts: 5.06 us -> 5.06 us
  transfers between devices with their start and end apart: 7 -> 6, of which waited for: 3 -> 3; matrix products, arithmetic and copies ran while one was open for 2% -> 1% of each run, Pallas kernels for 4% -> 3%
where the time goes in v3:
time: 125 us; the launch traced here: 123 us
  blocking collectives  60.9 us (49%)
  waiting for transfers between devices  32.6 us (26%)
  starting transfers between devices  15.1 us (12%)
  local copies, waits for them, and re-layouts  5.38 us (4%)
  Pallas kernels  5.24 us (4%)
  other arithmetic  2.06 us (2%)
    all_gather x1, blocking collectives, steps(): lax.all_gather(sent.reshape(pair, width * rows), 'high', axis=0, tiled=True)  60.9 us
    ppermute x1, waiting for transfers between devices, steps(): far_low = lax.ppermute(near[:half], z, up)  27.9 us
    all_to_all x1, starting transfers between devices, steps(): turned = lax.all_to_all(pair_output_gradient, z, 0, 0, tiled=True)  11.3 us
    unnamed x17, local copies, waits for them, and re-layouts  5.06 us
    pallas_call x1, Pallas kernels, ahead_call(): pl.pallas_call(ahead_kernel, out_shape=(jax.ShapeDtypeStruct((residues *...  3.88 us
    all_to_all x1, waiting for transfers between devices, steps(): turned = lax.all_to_all(pair_output_gradient, z, 0, 0, tiled=True)  3.42 us
  transfers between devices with their start and end apart: 6, of which 3 were waited for; matrix products, arithmetic and copies ran while one was open for 1% of the time, Pallas kernels for 3%

profile of v3, /device:TPU:38, one launch (start us, length us, event | category | flops | bytes accessed | tf_op | source)
XLA Modules:
  0.0 123.4 jit_solution(11033863640962017726)
XLA Ops:
  0.6 0.0 copy-start
  0.6 0.9 copy-done
  1.6 0.9 fusion.1
  2.5 0.1 reshape.52
  2.7 60.9 %all_gather.3.near_ref = bf16[128,3072]{1,0:T(8,128)(2,1)S(1)} all-gather(bf16[8,3072]{1,0:T(8,128)(2,1)S(1)} %reshape.52), channel_id=1, replica_groups=mesh['group'=4,'high'=16,'low'=2,'core'=2] {'high'}, dimensions={0}, use_global_device_ids=true | all-gather | bytes 835584 | tf_op jit(solution)/shard_map/all_gather | solution.py:194
  63.6 0.0 collective-permute-start.2
  63.6 11.3 %all-to-all-start = ((bf16[256,4,128]{2,1,0:T(4,128)(2,1)}), bf16[256,4,128]{2,1,0:T(4,128)(2,1)S(1)}, u32[]{:S(2)}, u32[]{:S(2)}) async-start(bf16[256,4,128]{2,1,0:T(4,128)(2,1)} %param.11), calls=%async_computation | async-start | bytes 524288 | tf_op jit(solution)/shard_map/all_to_all | solution.py:198
  74.9 1.1 broadcast_select_fusion
  76.0 0.3 collective-permute-start.3
  76.4 0.1 fusion.23
  76.4 1.2 collective-permute-start
  77.6 2.2 %collective-permute-start.1 = (bf16[64,3072]{1,0:T(8,128)(2,1)S(1)}, bf16[64,3072]{1,0:T(8,128)(2,1)S(1)}, u32[]{:S(2)}, u32[]{:S(2)}) collective-permute-start(bf16[64,3072]{1,0:T(8,128)(2,1)S(1)} %get-tuple-element.18), channel_id=1, source_target_pairs={{0,62},{2,0},{4,2},{6,4},{8,6},{10,8},{12,10},{14,12},{16,14},{18,... | collective-permute-start | bytes 1179656 | tf_op jit(solution)/shard_map/ppermute | solution.py:197
  79.8 0.0 copy-start.1
  79.8 0.2 fusion.11
  80.0 0.7 copy-done.1
  80.7 0.1 copy.10
  80.8 0.0 collective-permute-done.2
  80.9 0.0 collective-permute-done.3
  81.0 27.9 %collective-permute-done.far_low_ref = bf16[64,3072]{1,0:T(8,128)(2,1)S(1)} collective-permute-done((bf16[64,3072]{1,0:T(8,128)(2,1)S(1)}, bf16[64,3072]{1,0:T(8,128)(2,1)S(1)}, u32[]{:S(2)}, u32[]{:S(2)}) %collective-permute-start) | collective-permute-done | bytes 393248 | tf_op jit(solution)/shard_map/ppermute | solution.py:196
  108.9 0.0 collective-permute-done.1.far_high_ref
  108.9 0.0 copy-start.2
  108.9 0.7 copy-done.2
  109.5 3.9 %pair_ahead.1 = (f32[256,96]{1,0:T(8,128)S(1)}, f32[128,1024]{1,0:T(8,128)S(1)}, bf16[4096,96]{1,0:T(8,128)(2,1)S(1)}) custom-call(bf16[128,3072]{1,0:T(8,128)(2,1)S(1)} %all_gather.3.near_ref, bf16[64,3072]{1,0:T(8,128)(2,1)S(1)} %collective-permute-done.far_low_ref, bf16[64,3072]{1,0:T(8,128)(2,1)S(1)} %collective-permute-done.1.far_high_ref, ...), custom_call_target="tpu_custom_call" | custom-call | flops 3000000000 | bytes 4000000 | tf_op jit(solution)/shard_map/pair_ahead/pallas_call | solution.py:126
  113.4 0.0 copy-start.3
  113.4 0.8 copy-done.3
  114.2 3.4 %all-to-all-done = bf16[256,4,128]{2,1,0:T(4,128)(2,1)S(1)} async-done(((bf16[256,4,128]{2,1,0:T(4,128)(2,1)}), bf16[256,4,128]{2,1,0:T(4,128)(2,1)S(1)}, u32[]{:S(2)}, u32[]{:S(2)}) %all-to-all-start) | async-done | bytes 262176 | tf_op jit(solution)/shard_map/all_to_all | solution.py:198
  117.6 0.0 copy-start.4
  117.6 1.0 copy-done.4
  118.7 1.4 %pair_behind.1 = f32[256,96]{1,0:T(8,128)S(1)} custom-call(f32[128,1024]{1,0:T(8,128)S(1)} %copy-done.4, bf16[4096,96]{1,0:T(8,128)(2,1)S(1)} %get-tuple-element.11.right_table_ref, bf16[1024,128]{1,0:T(8,128)(2,1)S(1)} %bitcast.52, f32[1,128]{1,0:T(1,128)S(1)} %bitcast.54, bf16[32,8,4,128]{3,2,1,0:T(4,128)(2,1)S(1)} %bitcast.50), custom_call_target="tpu_custom_call" | custom-call | flops 2000000000 | bytes 4000000 | tf_op jit(solution)/shard_map/pair_behind/pallas_call | solution.py:155
  120.1 0.1 collective-permute-start.4
  120.3 1.3 %collective-permute-done.4 = f32[8,32,96]{2,1,0:T(8,128)S(1)} collective-permute-done((f32[8,32,96]{2,1,0:T(8,128)S(1)}, f32[8,32,96]{2,1,0:T(8,128)S(1)}, u32[]{:S(2)}, u32[]{:S(2)}) %collective-permute-start.4) | collective-permute-done | bytes 98336 | tf_op jit(solution)/shard_map/ppermute | solution.py:243
  121.6 0.0 copy-start.5
  121.6 0.0 copy-start.6
  121.6 0.7 fusion.17
  122.3 0.0 copy-done.5
  122.3 0.0 copy-done.6
  122.3 0.2 fusion
  122.6 0.8 copy.13
  (15 shorter events, 0.2 us)
Async XLA Ops:
  0.6 0.9 copy-start
  63.6 17.2 %collective-permute-start.2 = (bf16[4,64,96]{2,1,0:T(8,128)(2,1)S(1)}, bf16[4,64,96]{2,1,0:T(8,128)(2,1)S(1)}, u32[]{:S(2)}, u32[]{:S(2)}) collective-permute-start(bf16[4,64,96]{2,1,0:T(8,128)(2,1)S(1)} %fusion.1), channel_id=1, source_target_pairs={{0,1},{1,0},{2,3},{3,2},{4,5},{5,4},{6,7},{7,6},{8,9},{9,8},{10,11... | collective-permute-start | bytes 147464 | tf_op jit(solution)/shard_map/ppermute | solution.py:209
  63.6 54.0 %all-to-all-start = ((bf16[256,4,128]{2,1,0:T(4,128)(2,1)}), bf16[256,4,128]{2,1,0:T(4,128)(2,1)S(1)}, u32[]{:S(2)}, u32[]{:S(2)}) async-start(bf16[256,4,128]{2,1,0:T(4,128)(2,1)} %param.11), calls=%async_computation | async-start | bytes 524288 | tf_op jit(solution)/shard_map/all_to_all | solution.py:198
  76.0 4.9 %collective-permute-start.3 = (bf16[32,4,4,128]{3,2,1,0:T(4,128)(2,1)S(1)}, bf16[32,4,4,128]{3,2,1,0:T(4,128)(2,1)S(1)}, u32[]{:S(2)}, u32[]{:S(2)}) collective-permute-start(bf16[32,4,4,128]{3,2,1,0:T(4,128)(2,1)S(1)} %get-tuple-element.21), channel_id=1, source_target_pairs={{0,1},{1,0},{2,3},{3,2},{4,5},{5,4},{6,7},{7,6},{8,9},{9,8},{10,11... | collective-permute-start | bytes 393224 | tf_op jit(solution)/shard_map/ppermute | solution.py:217
  76.4 32.5 %collective-permute-start = (bf16[64,3072]{1,0:T(8,128)(2,1)S(1)}, bf16[64,3072]{1,0:T(8,128)(2,1)S(1)}, u32[]{:S(2)}, u32[]{:S(2)}) collective-permute-start(bf16[64,3072]{1,0:T(8,128)(2,1)S(1)} %get-tuple-element.19), channel_id=1, source_target_pairs={{0,2},{2,4},{4,6},{6,8},{8,10},{10,12},{12,14},{14,16},{16,18},{18... | collective-permute-start | bytes 1179656 | tf_op jit(solution)/shard_map/ppermute | solution.py:196
  77.6 31.3 %collective-permute-start.1 = (bf16[64,3072]{1,0:T(8,128)(2,1)S(1)}, bf16[64,3072]{1,0:T(8,128)(2,1)S(1)}, u32[]{:S(2)}, u32[]{:S(2)}) collective-permute-start(bf16[64,3072]{1,0:T(8,128)(2,1)S(1)} %get-tuple-element.18), channel_id=1, source_target_pairs={{0,62},{2,0},{4,2},{6,4},{8,6},{10,8},{12,10},{14,12},{16,14},{18,... | collective-permute-start | bytes 1179656 | tf_op jit(solution)/shard_map/ppermute | solution.py:197
  79.8 1.0 copy-start.1
  108.9 0.7 copy-start.2
  113.4 0.8 copy-start.3
  117.6 1.0 copy-start.4
  120.1 1.5 %collective-permute-start.4 = (f32[8,32,96]{2,1,0:T(8,128)S(1)}, f32[8,32,96]{2,1,0:T(8,128)S(1)}, u32[]{:S(2)}, u32[]{:S(2)}) collective-permute-start(f32[8,32,96]{2,1,0:T(8,128)S(1)} %pad_maximum_fusion.1), channel_id=1, source_target_pairs={{0,1},{1,0},{2,3},{3,2},{4,5},{5,4},{6,7},{7,6},{8,9},{9,8},{10,11... | collective-permute-start | bytes 294920 | tf_op jit(solution)/shard_map/ppermute | solution.py:243
  121.6 0.7 copy-start.5
  121.6 0.7 copy-start.6
